TPU v7x, 32 devices: a whole 2x2x4 slice. The times are simulated.
32 devices in a mesh: layer: 4 (over y, x), latent: 8 (over z, core).
Axes of the slice: x: 2, y: 2, z: 4, core: 2. Of those that a mesh axis runs over, the one named last changes fastest.
Arguments:
- tokens: bfloat16 [128, 16384], P('latent', 'layer'), may hold values from -6 to 6
- encoder_weight: bfloat16 [16384, 16384], P('layer', 'latent'), may hold values from -0.046875 to 0.046875
- encoder_bias: float32 [16384], P('latent'), may hold values from -3 to 3, as said below
- decoder_weight: bfloat16 [16384, 16384], P('latent', 'layer'), may hold values from -2 to 2
- decoder_bias: float32 [16384], P('layer'), may hold values from -12 to 12
Outputs:
- encoder_grad: bfloat16 [16384, 16384], P('layer', 'latent')
- decoder_grad: bfloat16 [16384, 16384], P('latent', 'layer')
Inputs may be any that keep to these rules, and one draw needn't show every extreme that they name: `encoder_bias`: mean about -0.5.
All inputs are finite; a program needn't handle non-finite values.
Results may differ from a plain program's by a relative error of at most 0.0059.
Values may be sent and summed in bfloat16 or wider, within the bound.
No kernel may reach another device: no remote copies, remote signals or barrier semaphores. Data moves between devices by JAX's collectives and lax.ppermute only.
A program may use at most 128 MiB of HBM per device.

v0:
```python
import jax
import jax.numpy as jnp
from jax import lax
from jax.sharding import PartitionSpec as P

L = 4
D = 4096
LOSS_SCALE = 0.0625
SPARSITY = 0.5
sharpness = 4.0
epsilon = 1e-06


def shards(tokens, encoder_weight, encoder_bias, decoder_weight, decoder_bias):
    rows_dev, width_dev = tokens.shape
    latents_dev = encoder_weight.shape[1]
    groups = lax.axis_size("layer")
    layer_index = lax.axis_index("layer") * width_dev // D
    wide = decoder_weight.astype(jnp.float32)
    squares_own = jnp.sum(wide * wide, axis=1)
    placed = jnp.where(jnp.arange(L)[:, None] == layer_index, squares_own[None, :], 0.0)
    squares = lax.psum(placed, "layer")
    row_norms = jnp.sqrt(squares + epsilon)
    weights_sum = jnp.sum(row_norms, axis=0)
    own_norm = lax.dynamic_slice_in_dim(row_norms, layer_index, 1, 0)[0]
    every_token = lax.all_gather(tokens, "latent", axis=0, tiled=True)
    partial_value = jnp.dot(every_token, encoder_weight, preferred_element_type=jnp.float32)
    share_width = latents_dev // groups
    offset = lax.axis_index("layer") * share_width
    preact = lax.psum_scatter(partial_value, "layer", scatter_dimension=1, tiled=True)
    preact = preact + lax.dynamic_slice_in_dim(encoder_bias, offset, share_width, 0)[None, :]
    hidden_share = (jax.nn.softplus(sharpness * preact) / sharpness).astype(jnp.bfloat16)
    hidden = lax.all_gather(hidden_share, "layer", axis=1, tiled=True)
    slopes = jax.nn.sigmoid(sharpness * preact)
    rebuilt = lax.psum(
        jnp.dot(hidden, decoder_weight, preferred_element_type=jnp.float32), "latent"
    )
    errors = rebuilt + decoder_bias[None, :] - every_token.astype(jnp.float32)
    error_grad = (LOSS_SCALE * errors).astype(jnp.bfloat16)
    back_terms = lax.dot_general(
        error_grad, decoder_weight, (((1,), (1,)), ((), ())), preferred_element_type=jnp.float32
    )
    summed = lax.psum_scatter(back_terms, "layer", scatter_dimension=1, tiled=True)
    penalty = lax.dynamic_slice_in_dim(weights_sum, offset, share_width, 0)
    grad_share = ((summed + LOSS_SCALE * SPARSITY * penalty[None, :]) * slopes).astype(jnp.bfloat16)
    pre_grad = lax.all_gather(grad_share, "layer", axis=1, tiled=True)
    encoder_grad = lax.dot_general(
        every_token, pre_grad, (((0,), (0,)), ((), ())), preferred_element_type=jnp.float32
    ).astype(jnp.bfloat16)
    totals = jnp.sum(hidden.astype(jnp.float32), axis=0)
    direct = lax.dot_general(
        hidden, error_grad, (((0,), (0,)), ((), ())), preferred_element_type=jnp.float32
    )
    sparse_term = wide * (LOSS_SCALE * SPARSITY * totals / own_norm)[:, None]
    decoder_grad = (direct + sparse_term).astype(jnp.bfloat16)
    return (encoder_grad, decoder_grad)


def solution(mesh):
    placed = (
        P("latent", "layer"),
        P("layer", "latent"),
        P("latent"),
        P("latent", "layer"),
        P("layer"),
    )
    return jax.shard_map(
        shards,
        mesh=mesh,
        in_specs=placed,
        out_specs=(P("layer", "latent"), P("latent", "layer")),
        check_vma=False,
    )
```

profile of v0, /device:TPU:0, one launch (start us, length us, event | category | flops | bytes accessed | tf_op | source)
XLA Modules:
  0.0 247.9 jit_solution(9035878231300968238)
XLA Ops:
  7.2 0.0 all-gather.2.cloned.1.call-start
  7.2 0.7 all-gather.2.cloned.1.call-update
  7.9 0.0 reduce-scatter.3.cloned.1.call-start
  7.9 26.6 %all-gather.2.cloned.1.call-done = bf16[128,4096]{1,0:T(8,128)(2,1)} async-done(((bf16[16,4096]{1,0:T(8,128)(2,1)}), bf16[128,4096]{1,0:T(8,128)(2,1)}) %all-gather.2.cloned.1.call-update) | async-done | bytes 1048592 | tf_op jit(solution)/shard_map/all_gather | solution.py:26
  34.6 9.4 %fusion.6 = f32[128,2048]{1,0:T(8,128)} fusion(bf16[128,4096]{1,0:T(8,128)(2,1)} %all-gather.2.cloned.1.call-done, bf16[4096,2048]{1,0:T(8,128)(2,1)} %param.6), kind=kOutput, calls=%fused_computation.20 | convolution fusion | flops 2147483648 | bytes 18874368 | tf_op jit(solution)/shard_map/dot_general | solution.py:27
  44.0 0.0 reduce-scatter.3.cloned.1.call-update
  44.0 0.0 all-reduce.2.cloned.1.call-start
  44.1 0.8 dynamic_slice.9
  44.8 26.9 %reduce-scatter.3.cloned.1.call-done = f32[128,512]{1,0:T(8,128)} async-done(((f32[128,2048]{1,0:T(8,128)}), f32[128,512]{1,0:T(8,128)}) %reduce-scatter.3.cloned.1.call-update) | async-done | bytes 262160 | tf_op jit(solution)/shard_map/reduce_scatter | solution.py:30
  71.7 1.1 fusion.4
  72.8 10.1 %all_gather.10 = bf16[128,2048]{1,0:T(8,128)(2,1)S(1)} all-gather(bf16[128,512]{1,0:T(8,128)(2,1)S(1)} %fusion.4), channel_id=1, replica_groups=mesh['layer'=4,'latent'=8] {'layer'}, dimensions={1}, use_global_device_ids=true | all-gather | bytes 655360 | tf_op jit(solution)/shard_map/all_gather | solution.py:33
  82.9 0.0 copy-start
  82.9 0.0 copy-start.2
  82.9 9.5 %fusion.7 = f32[128,4096]{1,0:T(8,128)} fusion(bf16[128,2048]{1,0:T(8,128)(2,1)S(1)} %all_gather.10, bf16[2048,4096]{1,0:T(8,128)(2,1)} %param.8), kind=kOutput, calls=%fused_computation.21 | convolution fusion | flops 2147483648 | bytes 19398656 | tf_op jit(solution)/shard_map/dot_general | solution.py:36
  92.4 0.0 all-reduce.2.cloned.1.call-update
  92.5 0.0 reduce-scatter.5.cloned.1.call-start
  92.5 7.4 %fusion = f32[2048]{0:T(1024)S(1)} fusion(bf16[2048,4096]{1,0:T(8,128)(2,1)} %param.8), kind=kLoop, calls=%fused_computation.2 | loop fusion | flops 25163776 | bytes 16785408 | tf_op jit(solution)/shard_map/reduce_sum | solution.py:20
  99.9 0.1 broadcast_select_fusion
  100.0 15.1 %psum.15 = f32[4,2048]{1,0:T(4,128)S(1)} all-reduce(f32[4,2048]{1,0:T(4,128)S(1)} %broadcast_select_fusion), channel_id=1, replica_groups=mesh['layer'=4,'latent'=8] {'layer'}, use_global_device_ids=true, to_apply=%region_4.5 | all-reduce | flops 8192 | bytes 65536 | tf_op jit(solution)/shard_map/psum | solution.py:22
  115.2 42.5 %all-reduce.2.cloned.1.call-done = f32[128,4096]{1,0:T(8,128)} async-done(((f32[128,4096]{1,0:T(8,128)}), f32[128,4096]{1,0:T(8,128)}) %all-reduce.2.cloned.1.call-update) | async-done | bytes 2097168 | tf_op jit(solution)/shard_map/psum | solution.py:35
  157.7 0.0 copy-done
  157.7 0.0 copy-done.2
  157.7 1.9 multiply_convert_fusion
  159.6 12.4 %fusion.8 = f32[128,2048]{1,0:T(8,128)} fusion(bf16[128,4096]{1,0:T(8,128)(2,1)S(1)} %multiply_convert_fusion, bf16[2048,4096]{1,0:T(8,128)(2,1)} %param.8), kind=kOutput, calls=%fused_computation.22 | convolution fusion | flops 2147483648 | bytes 18874368 | tf_op jit(solution)/shard_map/dot_general | solution.py:40
  172.0 0.0 reduce-scatter.5.cloned.1.call-update
  172.0 0.1 dynamic-slice_multiply_fusion
  172.1 0.1 convert_reduce_fusion
  172.2 0.0 copy-start.1
  172.2 12.0 %fusion.2 = bf16[2048,4096]{1,0:T(8,128)(2,1)} fusion(bf16[2048,4096]{1,0:T(8,128)(2,1)} %param.8, f32[2048]{0:T(1024)S(1)} %multiply_divide_fusion, bf16[128,2048]{1,0:T(8,128)(2,1)S(1)} %all_gather.10, bf16[128,4096]{1,0:T(8,128)(2,1)S(1)} %multiply_convert_fusion), kind=kOutput, calls=%fused_computation.4 | convolution fusion | flops 2181038080 | bytes 35135488 | tf_op jit(solution)/shard_map/dot_general | solution.py:51
  184.2 15.5 %reduce-scatter.5.cloned.1.call-done = f32[128,512]{1,0:T(8,128)} async-done(((f32[128,2048]{1,0:T(8,128)}), f32[128,512]{1,0:T(8,128)}) %reduce-scatter.5.cloned.1.call-update) | async-done | bytes 262160 | tf_op jit(solution)/shard_map/reduce_scatter | solution.py:43
  199.7 0.0 copy-done.1
  199.7 1.0 multiply_convert_fusion.1
  200.8 10.1 %all_gather.11 = bf16[128,2048]{1,0:T(8,128)(2,1)S(1)} all-gather(bf16[128,512]{1,0:T(8,128)(2,1)S(1)} %multiply_convert_fusion.1), channel_id=1, replica_groups=mesh['layer'=4,'latent'=8] {'layer'}, dimensions={1}, use_global_device_ids=true | all-gather | bytes 655360 | tf_op jit(solution)/shard_map/all_gather | solution.py:46
  210.8 8.1 %convert_bitcast_fusion = bf16[4096,2048]{0,1:T(8,128)(2,1)} fusion(bf16[128,2048]{1,0:T(8,128)(2,1)S(1)} %all_gather.11, bf16[128,4096]{1,0:T(8,128)(2,1)S(1)} %copy-done), kind=kOutput, calls=%fused_computation.5 | convolution fusion | flops 2155872256 | bytes 18350080 | tf_op jit(solution)/shard_map/dot_general | solution.py:47
  218.9 22.4 %copy.8 = bf16[4096,2048]{1,0:T(8,128)(2,1)} copy(bf16[4096,2048]{0,1:T(8,128)(2,1)} %convert_bitcast_fusion) | data formatting | bytes 33554432
  (4 shorter events, 0.1 us)
Async XLA Ops:
  7.2 27.4 %all-gather.2.cloned.1.call-start = ((), (), s32[]{:S(2)}) async-start(), calls=%async_computation.2 | async-start | bytes 1179648 | tf_op jit(solution)/shard_map/all_gather | solution.py:26
  7.9 63.8 %reduce-scatter.3.cloned.1.call-start = ((), (), s32[]{:S(2)}) async-start(), calls=%async_computation.3 | async-start | bytes 1310720 | tf_op jit(solution)/shard_map/reduce_scatter | solution.py:30
  44.0 113.7 %all-reduce.2.cloned.1.call-start = ((), (), s32[]{:S(2)}) async-start(), calls=%async_computation.4 | async-start | bytes 4194304 | tf_op jit(solution)/shard_map/psum | solution.py:35
  82.9 74.8 %copy-start = (bf16[128,4096]{1,0:T(8,128)(2,1)S(1)}, bf16[128,4096]{1,0:T(8,128)(2,1)}, u32[]{:S(2)}) copy-start(bf16[128,4096]{1,0:T(8,128)(2,1)} %all-gather.2.cloned.1.call-done) | copy-start | bytes 3145732
  82.9 74.8 %copy-start.2 = (f32[4096]{0:T(1024)S(1)}, f32[4096]{0:T(1024)}, u32[]{:S(2)}) copy-start(f32[4096]{0:T(1024)} %param.9) | copy-start | bytes 49156
  92.5 107.3 %reduce-scatter.5.cloned.1.call-start = ((), (), s32[]{:S(2)}) async-start(), calls=%async_computation.5 | async-start | bytes 1310720 | tf_op jit(solution)/shard_map/reduce_scatter | solution.py:43
  172.2 27.5 %copy-start.1 = (f32[128,512]{1,0:T(8,128)S(1)}, f32[128,512]{1,0:T(8,128)}, u32[]{:S(2)}) copy-start(f32[128,512]{1,0:T(8,128)} %reduce-scatter.3.cloned.1.call-done) | copy-start | bytes 786436
Sparse Core Ops, SparseCore 0:
  9.6 24.9 all-gather.1
  44.1 27.5 reduce-scatter.2
  92.6 65.0 all-reduce.1
  172.1 27.5 reduce-scatter.4
where the time goes:
time: 249 us; the launch traced here: 248 us
  waiting for transfers between devices  112 us (45%)
  matrix products  51.3 us (21%)
  blocking collectives  35.3 us (14%)
  local copies, waits for them, and re-layouts  23.2 us (9%)
  between operations  13.9 us (6%)
  other arithmetic  11.7 us (5%)
    psum x1, waiting for transfers between devices, shards(): lax.psum(jnp.dot(hidden, decoder_weight, preferred_element_type=jnp.float...  42.5 us
    reduce_scatter x1, waiting for transfers between devices, shards(): lax.psum_scatter(partial_value, 'layer', scatter_dimension=1, tiled=True)  26.9 us
    all_gather x1, waiting for transfers between devices, shards(): every_token = lax.all_gather(tokens, 'latent', axis=0, tiled=True)  26.6 us
    unnamed x7, local copies, waits for them, and re-layouts  22.4 us
    reduce_scatter x1, waiting for transfers between devices, shards(): lax.psum_scatter(back_terms, 'layer', scatter_dimension=1, tiled=True)  15.5 us
    psum x1, blocking collectives, shards(): squares = lax.psum(placed, 'layer')  15.1 us
    dot_general x1, matrix products, shards(): lax.dot_general(error_grad, decoder_weight, (((1,), (1,)), ((), ())), pre...  12.4 us
    dot_general x1, matrix products, shards(): lax.dot_general(hidden, error_grad, (((0,), (0,)), ((), ())), preferred_e...  12 us
  transfers between devices with their start and end apart: 4, of which 4 were waited for; matrix products, arithmetic and copies ran while one was open for 8% of the time, Pallas kernels for 0%

commit v1 on v0

--- a/solution.py
+++ b/solution.py
@@ -32,9 +32,9 @@
     hidden_share = (jax.nn.softplus(sharpness * preact) / sharpness).astype(jnp.bfloat16)
     hidden = lax.all_gather(hidden_share, "layer", axis=1, tiled=True)
     slopes = jax.nn.sigmoid(sharpness * preact)
-    rebuilt = lax.psum(
-        jnp.dot(hidden, decoder_weight, preferred_element_type=jnp.float32), "latent"
-    )
+    own = jnp.dot(hidden, decoder_weight, preferred_element_type=jnp.float32)
+    parts = lax.all_gather(own, "latent")
+    rebuilt = jnp.sum(parts, axis=0)
     errors = rebuilt + decoder_bias[None, :] - every_token.astype(jnp.float32)
     error_grad = (LOSS_SCALE * errors).astype(jnp.bfloat16)
     back_terms = lax.dot_general(

time: 249 us -> 342 us (1.37)
  waiting for transfers between devices: 112 us -> 197 us
  other arithmetic: 11.7 us -> 20.4 us
    all_gather x0 -> x1, waiting for transfers between devices: none -> 128 us  [shards(): parts = lax.all_gather(own, 'latent')]
    psum x1 -> x0, waiting for transfers between devices: 42.5 us -> none  [shards(): lax.psum(jnp.dot(hidden, decoder_weight, preferred_element_type=jnp.float...]
    reduce_sum x0 -> x1, other arithmetic: none -> 8.68 us  [shards(): rebuilt = jnp.sum(parts, axis=0)]
  transfers between devices with their start and end apart: 4 -> 4, of which waited for: 4 -> 4; matrix products, arithmetic and copies ran while one was open for 8% -> 6% of each run, Pallas kernels for 0% -> 0%
where the time goes in v1:
time: 342 us; the launch traced here: 341 us
  waiting for transfers between devices  197 us (58%)
  matrix products  51.3 us (15%)
  blocking collectives  35.4 us (10%)
  local copies, waits for them, and re-layouts  23.2 us (7%)
  other arithmetic  20.4 us (6%)
  between operations  13.9 us (4%)
    all_gather x1, waiting for transfers between devices, shards(): parts = lax.all_gather(own, 'latent')  128 us
    reduce_scatter x1, waiting for transfers between devices, shards(): lax.psum_scatter(partial_value, 'layer', scatter_dimension=1, tiled=True)  26.9 us
    all_gather x1, waiting for transfers between devices, shards(): every_token = lax.all_gather(tokens, 'latent', axis=0, tiled=True)  26.6 us
    unnamed x7, local copies, waits for them, and re-layouts  22.4 us
    psum x1, blocking collectives, shards(): squares = lax.psum(placed, 'layer')  15.2 us
    reduce_scatter x1, waiting for transfers between devices, shards(): lax.psum_scatter(back_terms, 'layer', scatter_dimension=1, tiled=True)  14.1 us
    dot_general x1, matrix products, shards(): lax.dot_general(error_grad, decoder_weight, (((1,), (1,)), ((), ())), pre...  12.4 us
    dot_general x1, matrix products, shards(): lax.dot_general(hidden, error_grad, (((0,), (0,)), ((), ())), preferred_e...  12 us
  transfers between devices with their start and end apart: 4, of which 4 were waited for; matrix products, arithmetic and copies ran while one was open for 6% of the time, Pallas kernels for 0%

profile of v1, /device:TPU:0, one launch (start us, length us, event | category | flops | bytes accessed | tf_op | source)
XLA Modules:
  0.0 341.0 jit_solution(1450849716740138458)
XLA Ops:
  7.2 0.0 all-gather.4.cloned.1.call-start
  7.2 0.7 all-gather.4.cloned.1.call-update
  7.9 0.0 reduce-scatter.3.cloned.1.call-start
  7.9 26.6 %all-gather.4.cloned.1.call-done = bf16[128,4096]{1,0:T(8,128)(2,1)} async-done(((bf16[16,4096]{1,0:T(8,128)(2,1)}), bf16[128,4096]{1,0:T(8,128)(2,1)}) %all-gather.4.cloned.1.call-update) | async-done | bytes 1048592 | tf_op jit(solution)/shard_map/all_gather | solution.py:26
  34.6 9.4 %fusion.6 = f32[128,2048]{1,0:T(8,128)} fusion(bf16[128,4096]{1,0:T(8,128)(2,1)} %all-gather.4.cloned.1.call-done, bf16[4096,2048]{1,0:T(8,128)(2,1)} %param.6), kind=kOutput, calls=%fused_computation.20 | convolution fusion | flops 2147483648 | bytes 18874368 | tf_op jit(solution)/shard_map/dot_general | solution.py:27
  44.0 0.0 reduce-scatter.3.cloned.1.call-update
  44.0 0.0 all-gather.6.cloned.1.call-start
  44.1 0.8 dynamic_slice.9
  44.8 26.9 %reduce-scatter.3.cloned.1.call-done = f32[128,512]{1,0:T(8,128)} async-done(((f32[128,2048]{1,0:T(8,128)}), f32[128,512]{1,0:T(8,128)}) %reduce-scatter.3.cloned.1.call-update) | async-done | bytes 262160 | tf_op jit(solution)/shard_map/reduce_scatter | solution.py:30
  71.7 1.1 fusion.4
  72.8 10.1 %all_gather.16 = bf16[128,2048]{1,0:T(8,128)(2,1)S(1)} all-gather(bf16[128,512]{1,0:T(8,128)(2,1)S(1)} %fusion.4), channel_id=1, replica_groups=mesh['layer'=4,'latent'=8] {'layer'}, dimensions={1}, use_global_device_ids=true | all-gather | bytes 655360 | tf_op jit(solution)/shard_map/all_gather | solution.py:33
  82.9 9.4 %fusion.7 = f32[128,4096]{1,0:T(8,128)} fusion(bf16[128,2048]{1,0:T(8,128)(2,1)S(1)} %all_gather.16, bf16[2048,4096]{1,0:T(8,128)(2,1)} %param.8), kind=kOutput, calls=%fused_computation.21 | convolution fusion | flops 2147483648 | bytes 19398656 | tf_op jit(solution)/shard_map/dot_general | solution.py:35
  92.3 0.0 all-gather.6.cloned.1.call-update
  92.4 0.0 reduce-scatter.5.cloned.1.call-start
  92.4 0.0 copy-start
  92.4 0.0 copy-start.2
  92.5 7.4 %fusion = f32[2048]{0:T(1024)S(1)} fusion(bf16[2048,4096]{1,0:T(8,128)(2,1)} %param.8), kind=kLoop, calls=%fused_computation.2 | loop fusion | flops 25163776 | bytes 16785408 | tf_op jit(solution)/shard_map/reduce_sum | solution.py:20
  99.9 0.1 broadcast_select_fusion
  99.9 15.2 %psum.7 = f32[4,2048]{1,0:T(4,128)S(1)} all-reduce(f32[4,2048]{1,0:T(4,128)S(1)} %broadcast_select_fusion), channel_id=1, replica_groups=mesh['layer'=4,'latent'=8] {'layer'}, use_global_device_ids=true, to_apply=%region_4.5 | all-reduce | flops 8192 | bytes 65536 | tf_op jit(solution)/shard_map/psum | solution.py:22
  115.2 128.4 %all-gather.6.cloned.1.call-done = f32[1024,4096]{1,0:T(8,128)} async-done(((f32[128,4096]{1,0:T(8,128)}), f32[1024,4096]{1,0:T(8,128)}) %all-gather.6.cloned.1.call-update) | async-done | bytes 16777232 | tf_op jit(solution)/shard_map/all_gather | solution.py:36
  243.6 8.7 %reduce_sum.36 = f32[128,4096]{1,0:T(8,128)} reduce(f32[8,128,4096]{2,1,0:T(8,128)} %bitcast.14, f32[]{:T(128)} %constant.34.clone.1), dimensions={0}, to_apply=%region_1.2 | reduce | flops 3670016 | bytes 18874372 | tf_op jit(solution)/shard_map/reduce_sum | solution.py:37
  252.3 0.0 copy-done
  252.3 0.0 copy-done.2
  252.3 1.9 multiply_convert_fusion
  254.2 12.4 %fusion.8 = f32[128,2048]{1,0:T(8,128)} fusion(bf16[128,4096]{1,0:T(8,128)(2,1)S(1)} %multiply_convert_fusion, bf16[2048,4096]{1,0:T(8,128)(2,1)} %param.8), kind=kOutput, calls=%fused_computation.22 | convolution fusion | flops 2147483648 | bytes 18874368 | tf_op jit(solution)/shard_map/dot_general | solution.py:40
  266.6 0.0 reduce-scatter.5.cloned.1.call-update
  266.6 0.1 dynamic-slice_multiply_fusion
  266.7 0.1 convert_reduce_fusion
  266.8 0.0 copy-start.1
  266.8 12.0 %fusion.2 = bf16[2048,4096]{1,0:T(8,128)(2,1)} fusion(bf16[2048,4096]{1,0:T(8,128)(2,1)} %param.8, f32[2048]{0:T(1024)S(1)} %multiply_divide_fusion, bf16[128,2048]{1,0:T(8,128)(2,1)S(1)} %all_gather.16, bf16[128,4096]{1,0:T(8,128)(2,1)S(1)} %multiply_convert_fusion), kind=kOutput, calls=%fused_computation.4 | convolution fusion | flops 2181038080 | bytes 35135488 | tf_op jit(solution)/shard_map/dot_general | solution.py:51
  278.8 14.1 %reduce-scatter.5.cloned.1.call-done = f32[128,512]{1,0:T(8,128)} async-done(((f32[128,2048]{1,0:T(8,128)}), f32[128,512]{1,0:T(8,128)}) %reduce-scatter.5.cloned.1.call-update) | async-done | bytes 262160 | tf_op jit(solution)/shard_map/reduce_scatter | solution.py:43
  292.9 0.0 copy-done.1
  292.9 1.0 multiply_convert_fusion.1
  293.9 10.1 %all_gather.19 = bf16[128,2048]{1,0:T(8,128)(2,1)S(1)} all-gather(bf16[128,512]{1,0:T(8,128)(2,1)S(1)} %multiply_convert_fusion.1), channel_id=1, replica_groups=mesh['layer'=4,'latent'=8] {'layer'}, dimensions={1}, use_global_device_ids=true | all-gather | bytes 655360 | tf_op jit(solution)/shard_map/all_gather | solution.py:46
  304.0 8.1 %convert_bitcast_fusion = bf16[4096,2048]{0,1:T(8,128)(2,1)} fusion(bf16[128,2048]{1,0:T(8,128)(2,1)S(1)} %all_gather.19, bf16[128,4096]{1,0:T(8,128)(2,1)S(1)} %copy-done), kind=kOutput, calls=%fused_computation.5 | convolution fusion | flops 2155872256 | bytes 18350080 | tf_op jit(solution)/shard_map/dot_general | solution.py:47
  312.1 22.4 %copy.8 = bf16[4096,2048]{1,0:T(8,128)(2,1)} copy(bf16[4096,2048]{0,1:T(8,128)(2,1)} %convert_bitcast_fusion) | data formatting | bytes 33554432
  (4 shorter events, 0.1 us)
Async XLA Ops:
  7.2 27.4 %all-gather.4.cloned.1.call-start = ((), (), s32[]{:S(2)}) async-start(), calls=%async_computation.2 | async-start | bytes 1179648 | tf_op jit(solution)/shard_map/all_gather | solution.py:26
  7.9 63.8 %reduce-scatter.3.cloned.1.call-start = ((), (), s32[]{:S(2)}) async-start(), calls=%async_computation.3 | async-start | bytes 1310720 | tf_op jit(solution)/shard_map/reduce_scatter | solution.py:30
  44.0 199.6 %all-gather.6.cloned.1.call-start = ((), (), s32[]{:S(2)}) async-start(), calls=%async_computation.5 | async-start | bytes 18874368 | tf_op jit(solution)/shard_map/all_gather | solution.py:36
  92.4 200.5 %reduce-scatter.5.cloned.1.call-start = ((), (), s32[]{:S(2)}) async-start(), calls=%async_computation.4 | async-start | bytes 1310720 | tf_op jit(solution)/shard_map/reduce_scatter | solution.py:43
  92.4 159.8 %copy-start = (bf16[128,4096]{1,0:T(8,128)(2,1)S(1)}, bf16[128,4096]{1,0:T(8,128)(2,1)}, u32[]{:S(2)}) copy-start(bf16[128,4096]{1,0:T(8,128)(2,1)} %all-gather.4.cloned.1.call-done) | copy-start | bytes 3145732
  92.4 159.8 %copy-start.2 = (f32[4096]{0:T(1024)S(1)}, f32[4096]{0:T(1024)}, u32[]{:S(2)}) copy-start(f32[4096]{0:T(1024)} %param.9) | copy-start | bytes 49156
  266.8 26.1 %copy-start.1 = (f32[128,512]{1,0:T(8,128)S(1)}, f32[128,512]{1,0:T(8,128)}, u32[]{:S(2)}) copy-start(f32[128,512]{1,0:T(8,128)} %reduce-scatter.3.cloned.1.call-done) | copy-start | bytes 786436
Sparse Core Ops, SparseCore 0:
  9.6 24.9 all-gather.3
  44.1 27.5 reduce-scatter.2
  92.5 151.0 all-gather.5
  266.7 26.0 reduce-scatter.4
